TPU v7x, 32 devices: a whole 2x2x4 slice. The times are simulated.
32 devices in a mesh: gx: 4 (over y, x), gy: 8 (over z, core).
Axes of the slice: x: 2, y: 2, z: 4, core: 2. Of those that a mesh axis runs over, the one named last changes fastest.
Arguments:
- tile_flux: bfloat16 [4, 12, 8, 131072], P(None, None, None, ('gx', 'gy')), may hold values from -6 to 6
- tile_frac: float32 [8, 131072], P(None, ('gx', 'gy')), may hold values from 0.02 to 1
- weights: bfloat16 [32, 7, 16, 256, 128], P(('gx', 'gy')), may hold values from -0.049804688 to 0.14941406
- block_row: int32 [32, 7, 16], P(('gx', 'gy')), may hold values from 0 to 47
- block_col: int32 [32, 7, 16], P(('gx', 'gy')), may hold values from 0 to 31
- send_counts: int32 [32, 7], P(('gx', 'gy')), may hold values from 1 to 16, as said below
Outputs:
- atm_flux: float32 [4, 12, 393216], P(None, None, ('gx', 'gy'))
Inputs may be any that keep to these rules, and one draw needn't show every extreme that they name: `send_counts`: live slots of a device at an offset; some device has all 7 offsets at 16, and some device receives 16 live slots from every offset.
All inputs are finite; a program needn't handle non-finite values.
Results may differ from a plain program's by a relative error of at most 0.0029.
Values sent between devices are 32-bit elements; how exact they have to be, the bound alone decides.
A program may use at most 128 MiB of HBM per device.

v0:
```python
import functools

import jax
import jax.numpy as jnp
from jax import lax
from jax.experimental import pallas as pl
from jax.experimental.pallas import tpu as pltpu
from jax.sharding import PartitionSpec as P

CUTS = 8
OUT_CUTS = 4
EARLY = 4


def chunk_spans(slots):
    spans, begin, size = [], 0, max(slots // CUTS, 1)
    while begin < slots:
        size = min(size if begin == 0 else begin, slots - begin)
        spans.append((begin, size))
        begin += size
    return spans


def send_order(reach, spans):
    order = []
    for away in range(reach, 0, -1):
        for chunk in range(len(spans)):
            order += [(reach + away, chunk), (reach - away, chunk)]
    return order + [(reach, chunk) for chunk in range(len(spans))]


def exchange_kernel(axes, sizes, spans, flux_ref, frac_ref, col_ref, count_ref, rows_ref,
                    weights_ref, arrived_ref, arrived_rows_ref,
                    flux_buf, frac_buf, weights_buf, part_buf, flux_sem, frac_sem, weight_sem,
                    own_sem, send_sem, recv_sem, row_send_sem, row_recv_sem):
    num_off, slots = weights_buf.shape[0], weights_buf.shape[1]
    num_steps, num_kinds, tiles, _ = flux_ref.shape
    cols = weights_buf.shape[3]
    reach = num_off // 2
    inner = sizes[1]
    count = sizes[0] * sizes[1]
    me = lax.axis_index(axes[0]) * inner + lax.axis_index(axes[1])
    order = send_order(reach, spans)

    def place(offset):
        there = lax.rem(me + offset - reach + count, count)
        return (there // inner, lax.rem(there, inner))

    barrier = pltpu.get_barrier_semaphore()
    for offset in range(num_off):
        if offset != reach:
            pl.semaphore_signal(barrier, inc=1, device_id=place(offset),
                                device_id_type=pl.DeviceIdType.MESH)

    land_loads = []
    for block in range(flux_buf.shape[0]):
        lanes = pl.ds(block * cols, cols)
        land_loads.append(pltpu.make_async_copy(
            flux_ref.at[:, :, :, lanes], flux_buf.at[block], flux_sem.at[block]))
        land_loads.append(pltpu.make_async_copy(
            frac_ref.at[:, lanes], frac_buf.at[block], frac_sem.at[block]))
    for load in land_loads:
        load.start()
    loads = {}
    for offset, chunk in order:
        span = pl.ds(*spans[chunk])
        loads[offset, chunk] = pltpu.make_async_copy(
            weights_ref.at[offset, span], weights_buf.at[offset, span],
            weight_sem.at[offset, chunk])
    for key in order[:EARLY]:
        loads[key].start()

    for load in land_loads:
        load.wait()
    for key in order[EARLY:]:
        loads[key].start()
    copies = []
    for offset, chunk in order:
        begin, size = spans[chunk]
        loads[offset, chunk].wait()
        part_ref = arrived_ref if offset == reach else part_buf

        def one_slot(slot, carry, offset=offset, part_ref=part_ref):
            live = jnp.where(slot < count_ref[0, offset], 1.0, 0.0).astype(jnp.float32)
            block = col_ref[offset, 0, slot]
            frac = frac_buf[block]
            flux = flux_buf[block].astype(jnp.float32)
            flux = jnp.stack([flux[step] for step in range(num_steps)], axis=1)
            flux = flux.reshape(num_steps * num_kinds, tiles, cols)
            merged = jnp.sum(flux * frac[None], axis=1) / jnp.sum(frac, axis=0, keepdims=True)
            value = lax.dot_general(merged.astype(jnp.bfloat16), weights_buf[offset, slot],
                                    (((1,), (1,)), ((), ())),
                                    preferred_element_type=jnp.float32)
            part_ref[offset, slot] = value * live
            return carry

        lax.fori_loop(begin, begin + size, one_slot, 0)
        if not copies:
            pl.semaphore_wait(barrier, num_off - 1)
        span = pl.ds(begin, size)
        if offset != reach:
            copy = pltpu.make_async_remote_copy(
                src_ref=part_buf.at[offset, span], dst_ref=arrived_ref.at[offset, span],
                send_sem=send_sem.at[offset, chunk], recv_sem=recv_sem.at[offset, chunk],
                device_id=place(offset), device_id_type=pl.DeviceIdType.MESH)
            copy.start()
            copies.append(copy)
        if chunk == 0:
            if offset != reach:
                copy = pltpu.make_async_remote_copy(
                    src_ref=rows_ref.at[offset], dst_ref=arrived_rows_ref.at[offset],
                    send_sem=row_send_sem.at[offset], recv_sem=row_recv_sem.at[offset],
                    device_id=place(offset), device_id_type=pl.DeviceIdType.MESH)
            else:
                copy = pltpu.make_async_copy(
                    rows_ref.at[reach], arrived_rows_ref.at[reach], own_sem)
            copy.start()
            copies.append(copy)
    for copy in copies:
        copy.wait()


def settle_kernel(rows_ref, arrived_ref, out_ref, rows, total, out_buf, load_sem, out_sem):
    num_off, slots = arrived_ref.shape[0], arrived_ref.shape[1]
    num_kinds, num_steps = out_ref.shape[0], out_ref.shape[1]
    blocks, _, block_rows = total.shape
    load = pltpu.make_async_copy(rows_ref, rows, load_sem)
    load.start()
    total[...] = jnp.zeros_like(total)
    load.wait()
    for offset in range(num_off):
        def one_slot(slot, carry, offset=offset):
            row = rows[offset, 0, slot]
            total[row] = total[row] + arrived_ref[offset, slot]
            return carry

        lax.fori_loop(0, slots, one_slot, 0, unroll=4)

    per_cut = blocks // OUT_CUTS
    stores = []
    for cut in range(OUT_CUTS):
        def one_block(block, carry):
            lanes = pl.ds(pl.multiple_of(block * block_rows, block_rows), block_rows)
            out_buf[:, :, lanes] = total[block].reshape(num_kinds, num_steps, block_rows)
            return carry

        lax.fori_loop(cut * per_cut, (cut + 1) * per_cut, one_block, 0, unroll=2)
        lanes = pl.ds(cut * per_cut * block_rows, per_cut * block_rows)
        store = pltpu.make_async_copy(
            out_buf.at[:, :, lanes], out_ref.at[:, :, lanes], out_sem.at[cut])
        store.start()
        stores.append(store)
    for store in stores:
        store.wait()


def on_device(axes, sizes, atm_blocks, tile_flux, tile_frac, weights, block_row, block_col,
              send_counts):
    num_steps, num_kinds = tile_flux.shape[0], tile_flux.shape[1]
    num_flux = num_steps * num_kinds
    num_off, slots, block_rows, block_cols = weights.shape[1:]
    tiles = tile_flux.shape[2]
    land_blocks = tile_flux.shape[3] // block_cols
    spans = chunk_spans(slots)
    rows = block_row.transpose(1, 0, 2)
    columns = block_col.transpose(1, 0, 2)

    vmem = pl.BlockSpec(memory_space=pltpu.VMEM)
    smem = pl.BlockSpec(memory_space=pltpu.SMEM)
    hbm = pl.BlockSpec(memory_space=pltpu.HBM)
    arrived, arrived_rows = pl.pallas_call(
        functools.partial(exchange_kernel, axes, sizes, spans),
        out_shape=(
            pltpu.VMEM((num_off, slots, num_flux, block_rows), jnp.float32),
            pltpu.VMEM(rows.shape, jnp.int32),
        ),
        in_specs=[hbm, hbm, smem, smem, hbm, hbm],
        out_specs=(vmem, vmem),
        scratch_shapes=[
            pltpu.VMEM((land_blocks, num_steps, num_kinds, tiles, block_cols), tile_flux.dtype),
            pltpu.VMEM((land_blocks, tiles, block_cols), tile_frac.dtype),
            pltpu.VMEM(weights.shape[1:], weights.dtype),
            pltpu.VMEM((num_off, slots, num_flux, block_rows), jnp.float32),
            pltpu.SemaphoreType.DMA((land_blocks,)),
            pltpu.SemaphoreType.DMA((land_blocks,)),
            pltpu.SemaphoreType.DMA((num_off, len(spans))),
            pltpu.SemaphoreType.DMA,
            pltpu.SemaphoreType.DMA((num_off, len(spans))),
            pltpu.SemaphoreType.DMA((num_off, len(spans))),
            pltpu.SemaphoreType.DMA((num_off,)),
            pltpu.SemaphoreType.DMA((num_off,)),
        ],
        compiler_params=pltpu.CompilerParams(collective_id=0, has_side_effects=True,
                                             vmem_limit_bytes=57 * 2**20),
        name="exchange",
    )(tile_flux, tile_frac, columns, send_counts, rows, weights[0])

    out = pl.pallas_call(
        settle_kernel,
        out_shape=jax.ShapeDtypeStruct((num_kinds, num_steps, atm_blocks * block_rows),
                                       jnp.float32),
        in_specs=[vmem, vmem],
        out_specs=hbm,
        scratch_shapes=[
            pltpu.SMEM(rows.shape, jnp.int32),
            pltpu.VMEM((atm_blocks, num_flux, block_rows), jnp.float32),
            pltpu.VMEM((num_kinds, num_steps, atm_blocks * block_rows), jnp.float32),
            pltpu.SemaphoreType.DMA,
            pltpu.SemaphoreType.DMA((OUT_CUTS,)),
        ],
        compiler_params=pltpu.CompilerParams(vmem_limit_bytes=16 * 2**20),
        name="settle",
    )(arrived_rows, arrived)
    return out.transpose(1, 0, 2)


AB_DEV = 48


def solution(mesh):
    axes = ("gx", "gy")
    sizes = (mesh.shape["gx"], mesh.shape["gy"])
    return jax.shard_map(
        functools.partial(on_device, axes, sizes, AB_DEV),
        mesh=mesh,
        in_specs=(
            P(None, None, None, ("gx", "gy")),
            P(None, ("gx", "gy")),
            P(("gx", "gy"), None, None, None, None),
            P(("gx", "gy"), None, None),
            P(("gx", "gy"), None, None),
            P(("gx", "gy"), None),
        ),
        out_specs=P(None, None, ("gx", "gy")),
        check_vma=False,
    )
```

profile of v0, /device:TPU:16, one launch (start us, length us, event | category | flops | bytes accessed | tf_op | source)
XLA Modules:
  0.0 110.4 jit_solution(7962684769681654232)
XLA Ops:
  0.0 107.5 %exchange.1 = (f32[7,16,48,256]{3,2,1,0:T(8,128)S(1)}, s32[7,1,16]{2,1,0:T(1,128)S(1)}) custom-call(bf16[4,12,8,4096]{3,2,1,0:T(8,128)(2,1)} %flux_ref.1, f32[8,4096]{1,0:T(8,128)} %frac_ref.1, s32[7,1,16]{2,1,0:T(1,128)} %bitcast.5, s32[1,7]{1,0:T(1,128)} %count_ref.1, s32[7,1,16]{2,1,0:T(1,128)} %bitcast.6, bf16[7,16,256,128]{3,2,1,0:T(8,128)(2,1)} %bitcast.4), custom_call_target="tpu_custom_call" | custom-call | tf_op jit(solution)/shard_map/exchange/pallas_call | solution.py:171
  107.5 2.9 %settle.1 = f32[12,4,12288]{2,1,0:T(4,128)} custom-call(s32[7,1,16]{2,1,0:T(1,128)S(1)} %get-tuple-element.7.rows_ref, f32[7,16,48,256]{3,2,1,0:T(8,128)S(1)} %get-tuple-element.8.arrived_ref), custom_call_target="tpu_custom_call" | custom-call | tf_op jit(solution)/shard_map/settle/pallas_call | solution.py:198
where the time goes:
time: 112 us; the launch traced here: 110 us
  Pallas kernels  110 us (98%)
    pallas_call x1, Pallas kernels, on_device(): pl.pallas_call(functools.partial(exchange_kernel, axes, sizes, spans), ou...  107 us
    pallas_call x1, Pallas kernels, on_device(): pl.pallas_call(settle_kernel, out_shape=jax.ShapeDtypeStruct((num_kinds,...  2.91 us

commit v1 on v0

v1 whole, which is shorter than its diff:
```python
import functools

import jax
import jax.numpy as jnp
from jax import lax
from jax.experimental import pallas as pl
from jax.experimental.pallas import tpu as pltpu
from jax.sharding import PartitionSpec as P

OUT_CUTS = 4
EARLY = 4
CLASSES = 16
LANES = 128
COUNT_LANE = 64
AB_DEV = 48


def ranges(begin, end, sizes):
    spans = []
    for size in sizes:
        size = min(size, end - begin)
        if size > 0:
            spans.append((begin, size))
            begin += size
    if begin < end:
        spans.append((begin, end - begin))
    return spans


def flow_order(reach):
    order = []
    for away in range(reach, 0, -1):
        order += [reach + away, reach - away]
    return order


def greet(me, count, place):
    barrier = pltpu.get_barrier_semaphore()

    def one(step, carry):
        pl.semaphore_signal(barrier, inc=1, device_id=place(lax.rem(me + step, count)),
                            device_id_type=pl.DeviceIdType.MESH)
        return carry

    lax.fori_loop(1, count, one, 0)
    return barrier


def exchange_kernel(axes, sizes, first, half, flux_ref, frac_ref, col_ref, count_ref, rows_ref,
                    weights_ref, part_ref, own_ref, arrived_ref, arrived_rows_ref, votes_ref,
                    pick_ref,
                    flux_buf, frac_buf, weights_buf, flux_sem, frac_sem, weight_sem,
                    own_sem, send_sem, recv_sem, row_send_sem, row_recv_sem,
                    vote_send_sem, vote_recv_sem):
    num_off, slots = weights_buf.shape[0], weights_buf.shape[1]
    num_steps, num_kinds, tiles, _ = flux_ref.shape
    cols = weights_buf.shape[3]
    reach = num_off // 2
    inner = sizes[1]
    count = sizes[0] * sizes[1]
    me = lax.axis_index(axes[0]) * inner + lax.axis_index(axes[1])
    first_spans = ranges(0, first, (1, 1, 2))
    later_spans = ranges(first, slots, (half - first,))

    def place(there):
        return (there // inner, lax.rem(there, inner))

    def target(offset):
        return lax.rem(me + offset - reach + count, count)

    barrier = greet(me, count, place)

    land_loads = []
    for block in range(flux_buf.shape[0]):
        lanes = pl.ds(block * cols, cols)
        land_loads.append(pltpu.make_async_copy(
            flux_ref.at[:, :, :, lanes], flux_buf.at[block], flux_sem.at[block]))
        land_loads.append(pltpu.make_async_copy(
            frac_ref.at[:, lanes], frac_buf.at[block], frac_sem.at[block]))
    for load in land_loads:
        load.start()
    order = [(offset, span) for span in first_spans for offset in flow_order(reach)]
    order += [(offset, span) for span in later_spans for offset in flow_order(reach)]
    order += [(reach, (0, slots))]
    loads = []
    for index, (offset, span) in enumerate(order):
        loads.append(pltpu.make_async_copy(
            weights_ref.at[offset, pl.ds(*span)], weights_buf.at[offset, pl.ds(*span)],
            weight_sem.at[index]))
    for load in loads[:EARLY]:
        load.start()

    lane = lax.broadcasted_iota(jnp.int32, (1, LANES), 1)
    mine = lax.rem(me, CLASSES)
    vote = jnp.where(lane <= CLASSES, 1, 0)
    for offset in range(num_off):
        live = count_ref[0, offset]
        if offset != reach:
            theirs = lax.rem(target(offset), CLASSES)
            fits = (lane == mine) | (lane == theirs) | (lane >= CLASSES) | (live <= half)
            vote = jnp.where(fits, vote, 0)
        vote = jnp.where(lane == COUNT_LANE + offset, live, vote)
    votes_ref[me] = vote

    for load in land_loads:
        load.wait()
    for load in loads[EARLY:]:
        load.start()

    def vote_copy(step):
        return pltpu.make_async_remote_copy(
            src_ref=votes_ref.at[me], dst_ref=votes_ref.at[me],
            send_sem=vote_send_sem.at[step], recv_sem=vote_recv_sem.at[step],
            device_id=place(lax.rem(me + step, count)), device_id_type=pl.DeviceIdType.MESH)

    def send_vote(step, carry):
        vote_copy(step).start()
        return carry

    def settle_vote(step, carry):
        source = lax.rem(me - step + count, count)
        pltpu.make_async_remote_copy(
            src_ref=votes_ref.at[me], dst_ref=votes_ref.at[source],
            send_sem=vote_send_sem.at[step], recv_sem=vote_recv_sem.at[step],
            device_id=place(source), device_id_type=pl.DeviceIdType.MESH).wait()
        return carry

    copies = []
    for index, (offset, span) in enumerate(order):
        begin, size = span
        loads[index].wait()

        def one_slot(slot, carry, offset=offset):
            block = col_ref[offset, 0, slot]
            frac = frac_buf[block]
            flux = flux_buf[block].astype(jnp.float32)
            flux = jnp.stack([flux[step] for step in range(num_steps)], axis=1)
            flux = flux.reshape(num_steps * num_kinds, tiles, cols)
            merged = jnp.sum(flux * frac[None], axis=1) / jnp.sum(frac, axis=0, keepdims=True)
            value = lax.dot_general(
                merged.astype(jnp.bfloat16), weights_buf[offset, slot],
                (((1,), (1,)), ((), ())), preferred_element_type=jnp.float32)
            if offset == reach:
                own_ref[slot] = value
            else:
                part_ref[offset, slot] = value
            return carry

        lax.fori_loop(begin, begin + size, one_slot, 0)
        if index == 0:
            pl.semaphore_wait(barrier, count - 1)
        if span in first_spans and offset != reach:
            chunk = first_spans.index(span)
            copy = pltpu.make_async_remote_copy(
                src_ref=part_ref.at[offset, pl.ds(begin, size)],
                dst_ref=arrived_ref.at[offset, pl.ds(begin, size)],
                send_sem=send_sem.at[offset, chunk], recv_sem=recv_sem.at[offset, chunk],
                device_id=place(target(offset)), device_id_type=pl.DeviceIdType.MESH)
            copy.start()
            copies.append(copy)
        if index == 0:
            lax.fori_loop(1, count, send_vote, 0)
        if begin == 0:
            if offset != reach:
                copy = pltpu.make_async_remote_copy(
                    src_ref=rows_ref.at[offset], dst_ref=arrived_rows_ref.at[offset],
                    send_sem=row_send_sem.at[offset], recv_sem=row_recv_sem.at[offset],
                    device_id=place(target(offset)), device_id_type=pl.DeviceIdType.MESH)
            else:
                copy = pltpu.make_async_copy(
                    rows_ref.at[reach], arrived_rows_ref.at[reach], own_sem)
            copy.start()
            copies.append(copy)
    lax.fori_loop(1, count, settle_vote, 0)
    agreed = jnp.min(votes_ref[:, 0, :], axis=0, keepdims=True)
    pick_ref[0] = jnp.min(jnp.where((agreed > 0) & (lane <= CLASSES), lane, CLASSES))
    for copy in copies:
        copy.wait()


def rest_kernel(axes, sizes, group, first, half, part_ref, arrived_ref, relay,
                base_send, base_recv, send_sem, recv_sem, pass_send, pass_recv,
                fwd_send, fwd_recv):
    num_off, slots = part_ref.shape[0], part_ref.shape[1]
    reach = num_off // 2
    outer, inner = sizes
    count = outer * inner
    x, y = lax.axis_index(axes[0]), lax.axis_index(axes[1])
    me = x * inner + y
    pieces = outer
    piece = (slots - half) // pieces

    def place(there):
        return (there // inner, lax.rem(there, inner))

    def shifted(device, offset):
        return lax.rem(device + offset - reach + count, count)

    def remote(src, dst, send, recv, device):
        return pltpu.make_async_remote_copy(
            src_ref=src, dst_ref=dst, send_sem=send, recv_sem=recv,
            device_id=device, device_id_type=pl.DeviceIdType.MESH)

    def hot(source, offset):
        goal = shifted(source, offset)
        return (lax.rem(source, CLASSES) == group) | (lax.rem(goal, CLASSES) == group)

    barrier = greet(me, count, place)
    pl.semaphore_wait(barrier, count - 1)

    def each_flow(act):
        def one(index, carry):
            away = reach - index // 2
            act(jnp.where(lax.rem(index, 2) == 0, reach + away, reach - away))
            return carry

        lax.fori_loop(0, 2 * reach, one, 0)

    def each_relay(act):
        def one(part, carry):
            source = lax.rem(x - part + outer, outer) * inner + y

            def flow(offset):
                @pl.when(hot(source, offset))
                def _():
                    act(offset, part, source)

            each_flow(flow)
            return carry

        lax.fori_loop(1, pieces, one, 0)

    ends = slots if group is None else half

    def base(offset):
        return remote(part_ref.at[offset, pl.ds(first, ends - first)],
                      arrived_ref.at[offset, pl.ds(0, ends - first)],
                      base_send.at[offset], base_recv.at[offset], place(shifted(me, offset)))

    if group is None:
        each_flow(lambda offset: base(offset).start())
        each_flow(lambda offset: base(offset).wait())
        return

    def direct(offset):
        return remote(part_ref.at[offset, pl.ds(half, piece)],
                      arrived_ref.at[offset, pl.ds(half - first, piece)],
                      send_sem.at[offset], recv_sem.at[offset], place(shifted(me, offset)))

    def detour(offset, part):
        return remote(part_ref.at[offset, pl.ds(half + part * piece, piece)],
                      relay.at[offset, part], pass_send.at[offset, part],
                      pass_recv.at[offset, part], (lax.rem(x + part, outer), y))

    def forward(offset, part, source):
        return remote(relay.at[offset, part],
                      arrived_ref.at[offset, pl.ds(half - first + part * piece, piece)],
                      fwd_send.at[offset, part], fwd_recv.at[offset, part],
                      place(shifted(source, offset)))

    def each_part(act):
        def one(part, carry):
            act(part)
            return carry

        lax.fori_loop(1, pieces, one, 0)

    def start_hot(offset):
        @pl.when(hot(me, offset))
        def _():
            each_part(lambda part: detour(offset, part).start())
            direct(offset).start()

    def pass_on(offset, part, source):
        detour(offset, part).wait_recv()
        forward(offset, part, source).start()

    def finish(offset):
        origin = lax.rem(me - offset + reach + count, count)

        @pl.when(hot(me, offset))
        def _():
            direct(offset).wait_send()
            each_part(lambda part: detour(offset, part).wait_send())

        @pl.when(hot(origin, offset))
        def _():
            direct(offset).wait_recv()
            each_part(lambda part: forward(offset, part, me).wait_recv())

        base(offset).wait()

    each_flow(start_hot)
    each_flow(lambda offset: base(offset).start())
    each_relay(pass_on)
    each_flow(finish)
    each_relay(lambda offset, part, source: forward(offset, part, source).wait_send())


def settle_kernel(axes, sizes, rows_ref, votes_ref, own_ref, low_ref, high_ref, out_ref,
                  rows, lives, total, out_buf, load_sem, live_sem, out_sem):
    num_off, first = low_ref.shape[0], low_ref.shape[1]
    reach = num_off // 2
    count = sizes[0] * sizes[1]
    me = lax.axis_index(axes[0]) * sizes[1] + lax.axis_index(axes[1])
    num_kinds, num_steps = out_ref.shape[0], out_ref.shape[1]
    blocks, _, block_rows = total.shape
    loads = [pltpu.make_async_copy(rows_ref, rows, load_sem)]
    for offset in range(num_off):
        source = lax.rem(me - offset + reach + count, count)
        loads.append(pltpu.make_async_copy(
            votes_ref.at[source], lives.at[offset], live_sem.at[offset]))
    for load in loads:
        load.start()
    total[...] = jnp.zeros_like(total)
    for load in loads:
        load.wait()
    for offset in range(num_off):
        live = lives[offset, 0, COUNT_LANE + offset]

        def add(slot, value, offset=offset):
            row = rows[offset, 0, slot]
            total[row] = total[row] + value

        def low_slot(slot, carry, offset=offset, add=add):
            add(slot, own_ref[slot] if offset == reach else low_ref[offset, slot])
            return carry

        def high_slot(slot, carry, offset=offset, add=add):
            add(slot, high_ref[offset, slot - first])
            return carry

        if offset == reach:
            lax.fori_loop(0, live, low_slot, 0)
        else:
            lax.fori_loop(0, jnp.minimum(live, first), low_slot, 0)
            lax.fori_loop(first, live, high_slot, 0)

    per_cut = blocks // OUT_CUTS
    stores = []
    for cut in range(OUT_CUTS):
        def one_block(block, carry):
            lanes = pl.ds(pl.multiple_of(block * block_rows, block_rows), block_rows)
            out_buf[:, :, lanes] = total[block].reshape(num_kinds, num_steps, block_rows)
            return carry

        lax.fori_loop(cut * per_cut, (cut + 1) * per_cut, one_block, 0, unroll=2)
        lanes = pl.ds(cut * per_cut * block_rows, per_cut * block_rows)
        store = pltpu.make_async_copy(
            out_buf.at[:, :, lanes], out_ref.at[:, :, lanes], out_sem.at[cut])
        store.start()
        stores.append(store)
    for store in stores:
        store.wait()


def on_device(axes, sizes, atm_blocks, tile_flux, tile_frac, weights, block_row, block_col,
              send_counts):
    num_steps, num_kinds = tile_flux.shape[0], tile_flux.shape[1]
    num_flux = num_steps * num_kinds
    num_off, slots, block_rows, block_cols = weights.shape[1:]
    tiles = tile_flux.shape[2]
    land_blocks = tile_flux.shape[3] // block_cols
    rows = block_row.transpose(1, 0, 2)
    columns = block_col.transpose(1, 0, 2)
    count = sizes[0] * sizes[1]
    half, first = slots // 2, slots // 4
    piece = (slots - half) // sizes[0]

    vmem = pl.BlockSpec(memory_space=pltpu.VMEM)
    smem = pl.BlockSpec(memory_space=pltpu.SMEM)
    hbm = pl.BlockSpec(memory_space=pltpu.HBM)
    dma = pltpu.SemaphoreType.DMA
    steps = 2 * slots * num_off
    part, own, low, arrived_rows, votes, pick = pl.pallas_call(
        functools.partial(exchange_kernel, axes, sizes, first, half),
        out_shape=(
            pltpu.VMEM((num_off, slots, num_flux, block_rows), jnp.float32),
            pltpu.VMEM((slots, num_flux, block_rows), jnp.float32),
            pltpu.VMEM((num_off, first, num_flux, block_rows), jnp.float32),
            pltpu.VMEM(rows.shape, jnp.int32),
            pltpu.VMEM((count, 1, LANES), jnp.int32),
            jax.ShapeDtypeStruct((1,), jnp.int32),
        ),
        in_specs=[hbm, hbm, smem, smem, hbm, hbm],
        out_specs=(vmem, vmem, vmem, vmem, vmem, smem),
        scratch_shapes=[
            pltpu.VMEM((land_blocks, num_steps, num_kinds, tiles, block_cols), tile_flux.dtype),
            pltpu.VMEM((land_blocks, tiles, block_cols), tile_frac.dtype),
            pltpu.VMEM(weights.shape[1:], weights.dtype),
            dma((land_blocks,)),
            dma((land_blocks,)),
            dma((steps,)),
            dma,
            dma((num_off, first)),
            dma((num_off, first)),
            dma((num_off,)),
            dma((num_off,)),
            dma((count,)),
            dma((count,)),
        ],
        compiler_params=pltpu.CompilerParams(collective_id=0, has_side_effects=True,
                                             vmem_limit_bytes=55 * 2**20),
        name="exchange",
    )(tile_flux, tile_frac, columns, send_counts, rows, weights[0])

    def settle(arrived_rows, votes, own, low, high):
        return pl.pallas_call(
            functools.partial(settle_kernel, axes, sizes),
            out_shape=jax.ShapeDtypeStruct((num_kinds, num_steps, atm_blocks * block_rows),
                                           jnp.float32),
            in_specs=[vmem] * 5,
            out_specs=hbm,
            scratch_shapes=[
                pltpu.SMEM(rows.shape, jnp.int32),
                pltpu.SMEM((num_off, 1, LANES), jnp.int32),
                pltpu.VMEM((atm_blocks, num_flux, block_rows), jnp.float32),
                pltpu.VMEM((num_kinds, num_steps, atm_blocks * block_rows), jnp.float32),
                dma,
                dma((num_off,)),
                dma((OUT_CUTS,)),
            ],
            compiler_params=pltpu.CompilerParams(vmem_limit_bytes=16 * 2**20),
            name="settle",
        )(arrived_rows, votes, own, low, high)

    def rest(group):
        def call(part, arrived_rows, votes, own, low):
            high = pl.pallas_call(
                functools.partial(rest_kernel, axes, sizes, group, first, half),
                out_shape=pltpu.VMEM((num_off, slots - first, num_flux, block_rows),
                                     jnp.float32),
                in_specs=[vmem],
                out_specs=vmem,
                scratch_shapes=[
                    pltpu.VMEM((num_off, sizes[0], piece, num_flux, block_rows), jnp.float32),
                ] + [dma((num_off,))] * 4 + [dma((num_off, sizes[0]))] * 4,
                compiler_params=pltpu.CompilerParams(
                    collective_id=CLASSES + 1 if group is None else 1 + group,
                    has_side_effects=True, vmem_limit_bytes=16 * 2**20),
                name="rest",
            )(part)
            return settle(arrived_rows, votes, own, low, high)
        return call

    groups = list(range(CLASSES)) + [None]
    out = lax.switch(pick[0], [rest(group) for group in groups],
                     part, arrived_rows, votes, own, low)
    return out.transpose(1, 0, 2)


def solution(mesh):
    axes = ("gx", "gy")
    sizes = (mesh.shape["gx"], mesh.shape["gy"])
    return jax.shard_map(
        functools.partial(on_device, axes, sizes, AB_DEV),
        mesh=mesh,
        in_specs=(
            P(None, None, None, ("gx", "gy")),
            P(None, ("gx", "gy")),
            P(("gx", "gy"), None, None, None, None),
            P(("gx", "gy"), None, None),
            P(("gx", "gy"), None, None),
            P(("gx", "gy"), None),
        ),
        out_specs=P(None, None, ("gx", "gy")),
        check_vma=False,
    )
```

time: 112 us -> 81.5 us (0.73)
  the two profiles are of different devices: /device:TPU:16 before, /device:TPU:8 now
where the time goes in v1:
time: 81.5 us; the launch traced here: 81.3 us
  Pallas kernels  80.2 us (98%)
  between operations  0.82 us (1%)
    pallas_call x1, Pallas kernels, call(): pl.pallas_call(functools.partial(rest_kernel, axes, sizes, group, first,...  40.8 us
    pallas_call x1, Pallas kernels, on_device(): pl.pallas_call(functools.partial(exchange_kernel, axes, sizes, first, hal...  35.8 us
    pallas_call x1, Pallas kernels, settle(): pl.pallas_call(functools.partial(settle_kernel, axes, sizes), out_shape=j...  3.55 us

profile of v1, /device:TPU:8, one launch (start us, length us, event | category | flops | bytes accessed | tf_op | source)
XLA Modules:
  0.0 81.3 jit_solution(13494981438580379233)
XLA Ops:
  0.0 35.8 %exchange.1 = (f32[7,16,48,256]{3,2,1,0:T(8,128)S(1)}, f32[16,48,256]{2,1,0:T(8,128)S(1)}, f32[7,4,48,256]{3,2,1,0:T(8,128)S(1)}, s32[7,1,16]{2,1,0:T(1,128)S(1)}, s32[32,1,128]{2,1,0:T(1,128)S(1)}, /*index=5*/s32[1]{0:T(128)}) custom-call(bf16[4,12,8,4096]{3,2,1,0:T(8,128)(2,1)} %flux_ref.1, f32[8,4096]{1,0:T(8,128)} %frac_ref.1, s32[7,1,16]{2,1,0:T(1,128)} %bitcast.6, ...), custom_call_target="tpu_custom_call" | custom-call | tf_op jit(solution)/shard_map/exchange/pallas_call | solution.py:375
  36.5 44.7 %conditional.1 = (f32[12,4,12288]{2,1,0:T(4,128)}) conditional(s32[]{:T(128)} %bitcast.3, (f32[7,16,48,256]{3,2,1,0:T(8,128)S(1)}, s32[7,1,16]{2,1,0:T(1,128)S(1)}, s32[32,1,128]{2,1,0:T(1,128)S(1)}, f32[16,48,256]{2,1,0:T(8,128)S(1)}, f32[7,4,48,256]{3,2,1,0:T(8,128)S(1)}) %tuple.56, ...), branch_computations={%region_0.0_spmd, %region_1.0_spmd, %region_2.0_spmd, %region_3.0_... | conditional | bytes 8 | solution.py:447
  36.5 40.8 %rest.19.high_ref = f32[7,12,48,256]{3,2,1,0:T(8,128)S(1)} custom-call(f32[7,16,48,256]{3,2,1,0:T(8,128)S(1)} %get-tuple-element.206.part_ref), custom_call_target="tpu_custom_call" | custom-call | tf_op jit(solution)/shard_map/cond/branch_2_fun/rest/pallas_call | solution.py:429
  77.3 3.5 %settle.19 = f32[12,4,12288]{2,1,0:T(4,128)} custom-call(s32[7,1,16]{2,1,0:T(1,128)S(1)} %get-tuple-element.195.rows_ref, s32[32,1,128]{2,1,0:T(1,128)S(1)} %get-tuple-element.196.votes_ref, f32[16,48,256]{2,1,0:T(8,128)S(1)} %get-tuple-element.197.own_ref, f32[7,4,48,256]{3,2,1,0:T(8,128)S(1)} %get-tuple-element.204.low_ref, ...), custom_call_target="tpu_custom_call" | custom-call | tf_op jit(solution)/shard_map/cond/branch_2_fun/settle/pallas_call | solution.py:408

commit v2 on v1

v2 whole, which is shorter than its diff:
```python
import functools

import jax
import jax.numpy as jnp
from jax import lax
from jax.experimental import pallas as pl
from jax.experimental.pallas import tpu as pltpu
from jax.sharding import PartitionSpec as P

OUT_CUTS = 4
EARLY = 4
MAX_CLASSES = 32
CORES = 2
LANES = 128
AB_DEV = 48


def ranges(begin, end, sizes):
    spans = []
    for size in sizes:
        size = min(size, end - begin)
        if size > 0:
            spans.append((begin, size))
            begin += size
    if begin < end:
        spans.append((begin, end - begin))
    return spans


def flow_order(reach):
    order = []
    for away in range(reach, 0, -1):
        order += [reach + away, reach - away]
    return order


def flip(index, bits):
    out, weight = index, 1
    while weight <= bits:
        if bits // weight % 2:
            out = out + weight - 2 * weight * lax.rem(index // weight, 2)
        weight *= 2
    return out


def exchange_kernel(axes, sizes, classes, first, half, flux_ref, frac_ref, col_ref, count_ref, rows_ref,
                    weights_ref, part_ref, own_ref, arrived_ref, arrived_meta_ref, pick_ref,
                    flux_buf, frac_buf, weights_buf, meta, column_votes, row_votes,
                    flux_sem, frac_sem, weight_sem, meta_sem, own_sem, send_sem, recv_sem,
                    meta_send_sem, meta_recv_sem, column_send_sem, column_recv_sem,
                    row_send_sem, row_recv_sem):
    num_off, slots = weights_buf.shape[0], weights_buf.shape[1]
    num_steps, num_kinds, tiles, _ = flux_ref.shape
    cols = weights_buf.shape[3]
    reach = num_off // 2
    outer, inner = sizes
    count = outer * inner
    x, y = lax.axis_index(axes[0]), lax.axis_index(axes[1])
    me = x * inner + y
    first_spans = ranges(0, first, (1, 1, 2))
    later_spans = ranges(first, slots, (half - first,))

    def place(there):
        return (there // inner, lax.rem(there, inner))

    def target(offset):
        return lax.rem(me + offset - reach + count, count)

    def steps(size, act):
        def one(step, carry):
            act(step)
            return carry

        lax.fori_loop(1, size, one, 0)

    barrier = pltpu.get_barrier_semaphore()
    greeted = 2 * reach + outer - 1 + inner - 1

    def greet(device):
        pl.semaphore_signal(barrier, inc=1, device_id=device,
                            device_id_type=pl.DeviceIdType.MESH)

    for offset in flow_order(reach):
        greet(place(target(offset)))
    steps(outer, lambda step: greet((lax.rem(x + step, outer), y)))
    steps(inner, lambda step: greet((x, lax.rem(y + step, inner))))

    land_loads = []
    for block in range(flux_buf.shape[0]):
        lanes = pl.ds(block * cols, cols)
        land_loads.append(pltpu.make_async_copy(
            flux_ref.at[:, :, :, lanes], flux_buf.at[block], flux_sem.at[block]))
        land_loads.append(pltpu.make_async_copy(
            frac_ref.at[:, lanes], frac_buf.at[block], frac_sem.at[block]))
    for load in land_loads:
        load.start()
    meta_loads = [pltpu.make_async_copy(rows_ref.at[offset], meta.at[offset, 0],
                                        meta_sem.at[offset]) for offset in range(num_off)]
    for load in meta_loads:
        load.start()
    order = [(offset, span) for span in first_spans for offset in flow_order(reach)]
    order += [(offset, span) for span in later_spans for offset in flow_order(reach)]
    order += [(reach, (0, slots))]
    loads = []
    for index, (offset, span) in enumerate(order):
        loads.append(pltpu.make_async_copy(
            weights_ref.at[offset, pl.ds(*span)], weights_buf.at[offset, pl.ds(*span)],
            weight_sem.at[index]))
    for load in loads[:EARLY]:
        load.start()

    lane = lax.broadcasted_iota(jnp.int32, (1, LANES), 1)
    mine = lax.rem(me, classes)
    vote = jnp.where(lane <= classes, 1, 0)
    for offset in range(num_off):
        live = count_ref[0, offset]
        meta[offset, 1] = jnp.full((1, slots), live, jnp.int32)
        if offset != reach:
            theirs = lax.rem(target(offset), classes)
            fits = (lane == mine) | (lane == theirs) | (lane >= classes) | (live <= half)
            vote = jnp.where(fits, vote, 0)
    column_votes[x] = vote

    for load in land_loads:
        load.wait()
    for load in loads[EARLY:]:
        load.start()

    def column_vote(step, source):
        return pltpu.make_async_remote_copy(
            src_ref=column_votes.at[x], dst_ref=column_votes.at[source],
            send_sem=column_send_sem.at[step], recv_sem=column_recv_sem.at[step],
            device_id=(lax.rem(x + step, outer), y), device_id_type=pl.DeviceIdType.MESH)

    def row_vote(step, source):
        return pltpu.make_async_remote_copy(
            src_ref=row_votes.at[y], dst_ref=row_votes.at[source],
            send_sem=row_send_sem.at[step], recv_sem=row_recv_sem.at[step],
            device_id=(x, lax.rem(y + step, inner)), device_id_type=pl.DeviceIdType.MESH)

    copies = []
    for index, (offset, span) in enumerate(order):
        begin, size = span
        loads[index].wait()

        def one_slot(slot, carry, offset=offset):
            block = col_ref[offset, 0, slot]
            frac = frac_buf[block]
            flux = flux_buf[block].astype(jnp.float32)
            flux = jnp.stack([flux[step] for step in range(num_steps)], axis=1)
            flux = flux.reshape(num_steps * num_kinds, tiles, cols)
            merged = jnp.sum(flux * frac[None], axis=1) / jnp.sum(frac, axis=0, keepdims=True)
            value = lax.dot_general(
                merged.astype(jnp.bfloat16), weights_buf[offset, slot],
                (((1,), (1,)), ((), ())), preferred_element_type=jnp.float32)
            if offset == reach:
                own_ref[slot] = value
            else:
                part_ref[offset, slot] = value
            return carry

        lax.fori_loop(begin, begin + size, one_slot, 0, unroll=2 if size % 2 == 0 else 1)
        if index == 0:
            pl.semaphore_wait(barrier, greeted)
        if span in first_spans and offset != reach:
            chunk = first_spans.index(span)
            copy = pltpu.make_async_remote_copy(
                src_ref=part_ref.at[offset, pl.ds(begin, size)],
                dst_ref=arrived_ref.at[offset, pl.ds(begin, size)],
                send_sem=send_sem.at[offset, chunk], recv_sem=recv_sem.at[offset, chunk],
                device_id=place(target(offset)), device_id_type=pl.DeviceIdType.MESH)
            copy.start()
            copies.append(copy)
        if index == 0:
            steps(outer, lambda step: column_vote(step, x).start())
            for load in meta_loads:
                load.wait()
        if begin == 0:
            if offset != reach:
                copy = pltpu.make_async_remote_copy(
                    src_ref=meta.at[offset], dst_ref=arrived_meta_ref.at[offset],
                    send_sem=meta_send_sem.at[offset], recv_sem=meta_recv_sem.at[offset],
                    device_id=place(target(offset)), device_id_type=pl.DeviceIdType.MESH)
            else:
                copy = pltpu.make_async_copy(
                    meta.at[reach], arrived_meta_ref.at[reach], own_sem)
            copy.start()
            copies.append(copy)
        if index == 4 * reach - 1:
            steps(outer, lambda step: column_vote(
                step, lax.rem(x - step + outer, outer)).wait())
            row_votes[y] = jnp.min(column_votes[:, 0, :], axis=0, keepdims=True)
            steps(inner, lambda step: row_vote(step, y).start())
    steps(inner, lambda step: row_vote(step, lax.rem(y - step + inner, inner)).wait())
    agreed = jnp.min(row_votes[:, 0, :], axis=0, keepdims=True)
    pick_ref[0] = jnp.min(jnp.where((agreed > 0) & (lane <= classes), lane, classes))
    for copy in copies:
        copy.wait()


def rest_kernel(axes, sizes, classes, group, first, half, detours, part_ref, arrived_ref, relay,
                early_send, early_recv, late_send, late_recv, send_sem, recv_sem,
                pass_send, pass_recv, fwd_send, fwd_recv):
    num_off, slots = part_ref.shape[0], part_ref.shape[1]
    reach = num_off // 2
    outer, inner = sizes
    count = outer * inner
    x, y = lax.axis_index(axes[0]), lax.axis_index(axes[1])
    me = x * inner + y
    middle = (first + half) // 2
    straight = slots - half - sum(size for _, size in detours)

    def place(there):
        return (there // inner, lax.rem(there, inner))

    def shifted(device, offset):
        return lax.rem(device + offset - reach + count, count)

    def origin(offset):
        return lax.rem(me - offset + reach + count, count)

    def remote(src, dst, send, recv, device):
        return pltpu.make_async_remote_copy(
            src_ref=src, dst_ref=dst, send_sem=send, recv_sem=recv,
            device_id=device, device_id_type=pl.DeviceIdType.MESH)

    def heavy(source, offset):
        goal = shifted(source, offset)
        return (lax.rem(source, classes) == group) | (lax.rem(goal, classes) == group)

    def near(source, offset):
        return source // CORES == shifted(source, offset) // CORES

    def hot(source, offset):
        return heavy(source, offset) & jnp.logical_not(near(source, offset))

    def close(source, offset):
        return heavy(source, offset) & near(source, offset)

    def each_flow(act):
        def one(index, carry):
            away = reach - index // 2
            act(jnp.where(lax.rem(index, 2) == 0, reach + away, reach - away))
            return carry

        lax.fori_loop(0, 2 * reach, one, 0)

    def span(offset, begin, end, send, recv):
        return remote(part_ref.at[offset, pl.ds(begin, end - begin)],
                      arrived_ref.at[offset, pl.ds(begin - first, end - begin)],
                      send.at[offset], recv.at[offset], place(shifted(me, offset)))

    def early(offset):
        return span(offset, first, slots if group is None else middle, early_send, early_recv)

    def late(offset):
        return span(offset, middle, half, late_send, late_recv)

    def direct(offset):
        return span(offset, half, half + straight, send_sem, recv_sem)

    def whole(offset):
        return span(offset, half, slots, send_sem, recv_sem)

    barrier = pltpu.get_barrier_semaphore()

    def greet(device):
        pl.semaphore_signal(barrier, inc=1, device_id=device,
                            device_id_type=pl.DeviceIdType.MESH)

    each_flow(lambda offset: greet(place(shifted(me, offset))))
    if group is None:
        pl.semaphore_wait(barrier, 2 * reach)
        each_flow(lambda offset: early(offset).start())
        each_flow(lambda offset: early(offset).wait())
        return

    routes, begin = [], half + straight
    for index, (bits, size) in enumerate(detours):
        routes.append((index, bits, begin, size))
        begin += size

    def detour(offset, route):
        index, bits, begin, size = route
        return remote(part_ref.at[offset, pl.ds(begin, size)],
                      relay.at[offset, pl.ds(begin - half, size)], pass_send.at[offset, index],
                      pass_recv.at[offset, index], (flip(x, bits), y))

    def forward(offset, route, source):
        index, bits, begin, size = route
        return remote(relay.at[offset, pl.ds(begin - half, size)],
                      arrived_ref.at[offset, pl.ds(begin - first, size)],
                      fwd_send.at[offset, index], fwd_recv.at[offset, index],
                      place(shifted(source, offset)))

    def greet_route(offset, total):
        here, there = hot(me, offset), hot(origin(offset), offset)
        for _, bits, _, _ in routes:
            source = flip(x, bits) * inner + y
            middleman = hot(source, offset)

            @pl.when(here | middleman)
            def _():
                greet((flip(x, bits), y))

            @pl.when(middleman)
            def _():
                greet(place(shifted(source, offset)))

            @pl.when(there)
            def _():
                begun = origin(offset)
                greet((flip(begun // inner, bits), lax.rem(begun, inner)))

            total = (total + jnp.where(here | middleman, 1, 0) + jnp.where(middleman, 1, 0)
                     + jnp.where(there, 1, 0))
        return total

    def greet_one(index, total):
        away = reach - index // 2
        return greet_route(jnp.where(lax.rem(index, 2) == 0, reach + away, reach - away), total)

    pl.semaphore_wait(barrier, lax.fori_loop(0, 2 * reach, greet_one, 2 * reach))

    def start_hot(offset):
        @pl.when(hot(me, offset))
        def _():
            for route in routes:
                detour(offset, route).start()
            direct(offset).start()

        @pl.when(close(me, offset))
        def _():
            whole(offset).start()

    def pass_on(offset):
        for route in routes:
            source = flip(x, route[1]) * inner + y

            @pl.when(hot(source, offset))
            def _(route=route, source=source):
                detour(offset, route).wait_recv()
                forward(offset, route, source).start()

    def finish(offset):
        early(offset).wait()
        late(offset).wait()

        @pl.when(close(me, offset))
        def _():
            whole(offset).wait_send()

        @pl.when(close(origin(offset), offset))
        def _():
            whole(offset).wait_recv()

        @pl.when(hot(me, offset))
        def _():
            direct(offset).wait_send()
            for route in routes:
                detour(offset, route).wait_send()

        @pl.when(hot(origin(offset), offset))
        def _():
            direct(offset).wait_recv()
            for route in routes:
                forward(offset, route, me).wait_recv()

        for route in routes:
            source = flip(x, route[1]) * inner + y

            @pl.when(hot(source, offset))
            def _(route=route, source=source):
                forward(offset, route, source).wait_send()

    each_flow(start_hot)
    each_flow(lambda offset: early(offset).start())
    each_flow(pass_on)
    each_flow(lambda offset: late(offset).start())
    each_flow(finish)


def settle_kernel(meta_ref, own_ref, low_ref, high_ref, out_ref, meta, total, out_buf,
                  load_sem, out_sem):
    num_off, first = low_ref.shape[0], low_ref.shape[1]
    reach = num_off // 2
    num_kinds, num_steps = out_ref.shape[0], out_ref.shape[1]
    blocks, _, block_rows = total.shape
    load = pltpu.make_async_copy(meta_ref, meta, load_sem)
    load.start()

    def clear(block, carry):
        total[block] = jnp.zeros_like(total[block])
        return carry

    lax.fori_loop(0, blocks, clear, 0, unroll=4)
    load.wait()

    def add(offset, slot, value):
        row = meta[offset, 0, 0, slot]
        total[row] = total[row] + value

    def one_flow(offset, carry):
        live = meta[offset, 1, 0, 0]

        def low_slot(slot, carry):
            add(offset, slot, low_ref[offset, slot])
            return carry

        def high_slot(slot, carry):
            add(offset, slot, high_ref[offset, slot - first])
            return carry

        @pl.when(offset != reach)
        def _():
            lax.fori_loop(0, jnp.minimum(live, first), low_slot, 0)
            lax.fori_loop(first, live, high_slot, 0)

        return carry

    def own_slot(slot, carry):
        add(reach, slot, own_ref[slot])
        return carry

    lax.fori_loop(0, num_off, one_flow, 0)
    lax.fori_loop(0, meta[reach, 1, 0, 0], own_slot, 0)

    per_cut = blocks // OUT_CUTS
    stores = []
    for cut in range(OUT_CUTS):
        def one_block(block, carry):
            lanes = pl.ds(pl.multiple_of(block * block_rows, block_rows), block_rows)
            out_buf[:, :, lanes] = total[block].reshape(num_kinds, num_steps, block_rows)
            return carry

        lax.fori_loop(cut * per_cut, (cut + 1) * per_cut, one_block, 0, unroll=2)
        lanes = pl.ds(cut * per_cut * block_rows, per_cut * block_rows)
        store = pltpu.make_async_copy(
            out_buf.at[:, :, lanes], out_ref.at[:, :, lanes], out_sem.at[cut])
        store.start()
        stores.append(store)
    for store in stores:
        store.wait()


def on_device(axes, sizes, atm_blocks, tile_flux, tile_frac, weights, block_row, block_col,
              send_counts):
    num_steps, num_kinds = tile_flux.shape[0], tile_flux.shape[1]
    num_flux = num_steps * num_kinds
    num_off, slots, block_rows, block_cols = weights.shape[1:]
    tiles = tile_flux.shape[2]
    land_blocks = tile_flux.shape[3] // block_cols
    rows = block_row.transpose(1, 0, 2)
    columns = block_col.transpose(1, 0, 2)
    count = sizes[0] * sizes[1]
    half, first = slots // 2, slots // 4
    share = (slots - half) // 8
    detours = ((1, 2 * share), (2, 3 * share)) if sizes[0] % 4 == 0 else ()
    classes = min(count, MAX_CLASSES)

    vmem = pl.BlockSpec(memory_space=pltpu.VMEM)
    smem = pl.BlockSpec(memory_space=pltpu.SMEM)
    hbm = pl.BlockSpec(memory_space=pltpu.HBM)
    dma = pltpu.SemaphoreType.DMA
    steps = 2 * slots * num_off
    part, own, low, arrived_meta, pick = pl.pallas_call(
        functools.partial(exchange_kernel, axes, sizes, classes, first, half),
        out_shape=(
            pltpu.VMEM((num_off, slots, num_flux, block_rows), jnp.float32),
            pltpu.VMEM((slots, num_flux, block_rows), jnp.float32),
            pltpu.VMEM((num_off, first, num_flux, block_rows), jnp.float32),
            pltpu.VMEM((num_off, 2, 1, slots), jnp.int32),
            jax.ShapeDtypeStruct((1,), jnp.int32),
        ),
        in_specs=[hbm, hbm, smem, smem, hbm, hbm],
        out_specs=(vmem, vmem, vmem, vmem, smem),
        scratch_shapes=[
            pltpu.VMEM((land_blocks, num_steps, num_kinds, tiles, block_cols), tile_flux.dtype),
            pltpu.VMEM((land_blocks, tiles, block_cols), tile_frac.dtype),
            pltpu.VMEM(weights.shape[1:], weights.dtype),
            pltpu.VMEM((num_off, 2, 1, slots), jnp.int32),
            pltpu.VMEM((sizes[0], 1, LANES), jnp.int32),
            pltpu.VMEM((sizes[1], 1, LANES), jnp.int32),
            dma((land_blocks,)),
            dma((land_blocks,)),
            dma((steps,)),
            dma((num_off,)),
            dma,
            dma((num_off, first)),
            dma((num_off, first)),
            dma((num_off,)),
            dma((num_off,)),
            dma((sizes[0],)),
            dma((sizes[0],)),
            dma((sizes[1],)),
            dma((sizes[1],)),
        ],
        compiler_params=pltpu.CompilerParams(collective_id=0, has_side_effects=True,
                                             vmem_limit_bytes=55 * 2**20),
        name="exchange",
    )(tile_flux, tile_frac, columns, send_counts, rows, weights[0])

    def settle(arrived_meta, own, low, high):
        return pl.pallas_call(
            settle_kernel,
            out_shape=jax.ShapeDtypeStruct((num_kinds, num_steps, atm_blocks * block_rows),
                                           jnp.float32),
            in_specs=[vmem] * 4,
            out_specs=hbm,
            scratch_shapes=[
                pltpu.SMEM((num_off, 2, 1, slots), jnp.int32),
                pltpu.VMEM((atm_blocks, num_flux, block_rows), jnp.float32),
                pltpu.VMEM((num_kinds, num_steps, atm_blocks * block_rows), jnp.float32),
                dma,
                dma((OUT_CUTS,)),
            ],
            compiler_params=pltpu.CompilerParams(vmem_limit_bytes=16 * 2**20),
            name="settle",
        )(arrived_meta, own, low, high)

    def rest(group):
        def call(part, arrived_meta, own, low):
            high = pl.pallas_call(
                functools.partial(rest_kernel, axes, sizes, classes, group, first, half, detours),
                out_shape=pltpu.VMEM((num_off, slots - first, num_flux, block_rows),
                                     jnp.float32),
                in_specs=[vmem],
                out_specs=vmem,
                scratch_shapes=[
                    pltpu.VMEM((num_off, slots - half, num_flux, block_rows), jnp.float32),
                ] + [dma((num_off,))] * 6 + [dma((num_off, max(len(detours), 1)))] * 4,
                compiler_params=pltpu.CompilerParams(
                    collective_id=classes + 1 if group is None else 1 + group,
                    has_side_effects=True, vmem_limit_bytes=16 * 2**20),
                name="rest",
            )(part)
            return settle(arrived_meta, own, low, high)
        return call

    groups = list(range(classes)) + [None]
    out = lax.switch(pick[0], [rest(group) for group in groups],
                     part, arrived_meta, own, low)
    return out.transpose(1, 0, 2)


def solution(mesh):
    axes = ("gx", "gy")
    sizes = (mesh.shape["gx"], mesh.shape["gy"])
    return jax.shard_map(
        functools.partial(on_device, axes, sizes, AB_DEV),
        mesh=mesh,
        in_specs=(
            P(None, None, None, ("gx", "gy")),
            P(None, ("gx", "gy")),
            P(("gx", "gy"), None, None, None, None),
            P(("gx", "gy"), None, None),
            P(("gx", "gy"), None, None),
            P(("gx", "gy"), None),
        ),
        out_specs=P(None, None, ("gx", "gy")),
        check_vma=False,
    )
```

time: 81.5 us -> 73.8 us (0.906)
  the two profiles are of different devices: /device:TPU:8 before, /device:TPU:16 now
where the time goes in v2:
time: 73.8 us; the launch traced here: 72.7 us
  Pallas kernels  71.6 us (97%)
  between operations  0.82 us (1%)
    pallas_call x1, Pallas kernels, on_device(): pl.pallas_call(functools.partial(exchange_kernel, axes, sizes, classes, f...  34.5 us
    pallas_call x1, Pallas kernels, call(): pl.pallas_call(functools.partial(rest_kernel, axes, sizes, classes, group...  34.4 us
    pallas_call x1, Pallas kernels, settle(): pl.pallas_call(settle_kernel, out_shape=jax.ShapeDtypeStruct((num_kinds,...  2.73 us

profile of v2, /device:TPU:16, one launch (start us, length us, event | category | flops | bytes accessed | tf_op | source)
XLA Modules:
  0.0 72.7 jit_solution(13787058919669926228)
XLA Ops:
  0.0 34.5 %exchange.1 = (f32[7,16,48,256]{3,2,1,0:T(8,128)S(1)}, f32[16,48,256]{2,1,0:T(8,128)S(1)}, f32[7,4,48,256]{3,2,1,0:T(8,128)S(1)}, s32[7,2,1,16]{3,2,1,0:T(1,128)S(1)}, s32[1]{0:T(128)}) custom-call(bf16[4,12,8,4096]{3,2,1,0:T(8,128)(2,1)} %flux_ref.1, f32[8,4096]{1,0:T(8,128)} %frac_ref.1, s32[7,1,16]{2,1,0:T(1,128)} %bitcast.6, s32[1,7]{1,0:T(1,128)} %count_ref.1, ...), custom_call_target="tpu_custom_call" | custom-call | tf_op jit(solution)/shard_map/exchange/pallas_call | solution.py:466
  35.1 37.4 %conditional.1 = (f32[12,4,12288]{2,1,0:T(4,128)}) conditional(s32[]{:T(128)} %bitcast.3, (f32[7,16,48,256]{3,2,1,0:T(8,128)S(1)}, s32[7,2,1,16]{3,2,1,0:T(1,128)S(1)}, f32[16,48,256]{2,1,0:T(8,128)S(1)}, f32[7,4,48,256]{3,2,1,0:T(8,128)S(1)}) %tuple.104, (f32[7,16,48,256]{3,2,1,0:T(8,128)S(1)}, ...), branch_computations={%region_0.0_spmd, %region_1.0_spmd, %region_2.0_spmd, %region_3.0_... | conditional | bytes 8 | solution.py:541
  35.1 34.4 %rest.35.high_ref = f32[7,12,48,256]{3,2,1,0:T(8,128)S(1)} custom-call(f32[7,16,48,256]{3,2,1,0:T(8,128)S(1)} %get-tuple-element.292.part_ref), custom_call_target="tpu_custom_call" | custom-call | tf_op jit(solution)/shard_map/cond/branch_2_fun/rest/pallas_call | solution.py:523
  69.5 2.7 %settle.35 = f32[12,4,12288]{2,1,0:T(4,128)} custom-call(s32[7,2,1,16]{3,2,1,0:T(1,128)S(1)} %get-tuple-element.284.meta_ref, f32[16,48,256]{2,1,0:T(8,128)S(1)} %get-tuple-element.290.own_ref, f32[7,4,48,256]{3,2,1,0:T(8,128)S(1)} %get-tuple-element.291.low_ref, f32[7,12,48,256]{3,2,1,0:T(8,128)S(1)} %rest.35.high_ref), custom_call_target="tpu_custom_call" | custom-call | tf_op jit(solution)/shard_map/cond/branch_2_fun/settle/pallas_call | solution.py:504

commit v3 on v2

--- a/solution.py
+++ b/solution.py
@@ -34,11 +34,11 @@
     return order
 
 
-def flip(index, bits):
+def flip(index, bits, size):
     out, weight = index, 1
-    while weight <= bits:
-        if bits // weight % 2:
-            out = out + weight - 2 * weight * lax.rem(index // weight, 2)
+    while weight < size:
+        mine, theirs = lax.rem(index // weight, 2), lax.rem(bits // weight, 2)
+        out = out + weight * theirs * (1 - 2 * mine)
         weight *= 2
     return out
 
@@ -198,17 +198,17 @@
         copy.wait()
 
 
-def rest_kernel(axes, sizes, classes, group, first, half, detours, part_ref, arrived_ref, relay,
-                early_send, early_recv, late_send, late_recv, send_sem, recv_sem,
-                pass_send, pass_recv, fwd_send, fwd_recv):
+def rest_kernel(axes, sizes, classes, group, first, half, parts, part_ref, arrived_ref, relay,
+                base_send, base_recv, send_sem, recv_sem, pass_send, pass_recv,
+                fwd_send, fwd_recv):
     num_off, slots = part_ref.shape[0], part_ref.shape[1]
     reach = num_off // 2
     outer, inner = sizes
     count = outer * inner
     x, y = lax.axis_index(axes[0]), lax.axis_index(axes[1])
     me = x * inner + y
-    middle = (first + half) // 2
-    straight = slots - half - sum(size for _, size in detours)
+    batch = (half - first) // 2
+    piece = (slots - half) // parts
 
     def place(there):
         return (there // inner, lax.rem(there, inner))
@@ -218,90 +218,102 @@
 
     def origin(offset):
         return lax.rem(me - offset + reach + count, count)
+
+    def beside(part):
+        return flip(x, part, outer)
 
     def remote(src, dst, send, recv, device):
         return pltpu.make_async_remote_copy(
             src_ref=src, dst_ref=dst, send_sem=send, recv_sem=recv,
             device_id=device, device_id_type=pl.DeviceIdType.MESH)
 
-    def heavy(source, offset):
+    def member(device):
+        return (device if classes == count else lax.rem(device, classes)) == group
+
+    def heavy(source, goal):
+        return member(source) | member(goal)
+
+    def near(source, goal):
+        return source // CORES == goal // CORES
+
+    def hot(source, offset):
         goal = shifted(source, offset)
-        return (lax.rem(source, classes) == group) | (lax.rem(goal, classes) == group)
-
-    def near(source, offset):
-        return source // CORES == shifted(source, offset) // CORES
-
-    def hot(source, offset):
-        return heavy(source, offset) & jnp.logical_not(near(source, offset))
+        return heavy(source, goal) & jnp.logical_not(near(source, goal))
 
     def close(source, offset):
-        return heavy(source, offset) & near(source, offset)
+        goal = shifted(source, offset)
+        return heavy(source, goal) & near(source, goal)
+
+    def repeat(begin, end, act):
+        def one(step, carry):
+            act(step)
+            return carry
+
+        lax.fori_loop(begin, end, one, 0)
 
     def each_flow(act):
-        def one(index, carry):
+        def one(index):
             away = reach - index // 2
             act(jnp.where(lax.rem(index, 2) == 0, reach + away, reach - away))
-            return carry
-
-        lax.fori_loop(0, 2 * reach, one, 0)
-
-    def span(offset, begin, end, send, recv):
-        return remote(part_ref.at[offset, pl.ds(begin, end - begin)],
-                      arrived_ref.at[offset, pl.ds(begin - first, end - begin)],
-                      send.at[offset], recv.at[offset], place(shifted(me, offset)))
-
-    def early(offset):
-        return span(offset, first, slots if group is None else middle, early_send, early_recv)
-
-    def late(offset):
-        return span(offset, middle, half, late_send, late_recv)
+
+        repeat(0, 2 * reach, one)
+
+    def each_part(act):
+        repeat(1, parts, act)
+
+    def span(offset, begin, size, send, recv):
+        return remote(part_ref.at[offset, pl.ds(begin, size)],
+                      arrived_ref.at[offset, pl.ds(begin - first, size)],
+                      send, recv, place(shifted(me, offset)))
+
+    def base(offset, step):
+        size = slots - first if group is None else batch
+        return span(offset, first + step * batch, size, base_send.at[offset, step],
+                    base_recv.at[offset, step])
 
     def direct(offset):
-        return span(offset, half, half + straight, send_sem, recv_sem)
+        return span(offset, half, piece, send_sem.at[offset], recv_sem.at[offset])
 
     def whole(offset):
-        return span(offset, half, slots, send_sem, recv_sem)
+        return span(offset, half, slots - half, send_sem.at[offset], recv_sem.at[offset])
+
+    def detour(offset, part):
+        return remote(part_ref.at[offset, pl.ds(half + part * piece, piece)],
+                      relay.at[offset, part], pass_send.at[offset, part],
+                      pass_recv.at[offset, part], (beside(part), y))
+
+    def forward(offset, part, source):
+        return remote(relay.at[offset, part],
+                      arrived_ref.at[offset, pl.ds(half - first + part * piece, piece)],
+                      fwd_send.at[offset, part], fwd_recv.at[offset, part],
+                      place(shifted(source, offset)))
 
     barrier = pltpu.get_barrier_semaphore()
 
-    def greet(device):
-        pl.semaphore_signal(barrier, inc=1, device_id=device,
+    def greet(device, inc=1):
+        pl.semaphore_signal(barrier, inc=inc, device_id=device,
                             device_id_type=pl.DeviceIdType.MESH)
 
     each_flow(lambda offset: greet(place(shifted(me, offset))))
     if group is None:
         pl.semaphore_wait(barrier, 2 * reach)
-        each_flow(lambda offset: early(offset).start())
-        each_flow(lambda offset: early(offset).wait())
+        each_flow(lambda offset: base(offset, 0).start())
+        each_flow(lambda offset: base(offset, 0).wait())
         return
 
-    routes, begin = [], half + straight
-    for index, (bits, size) in enumerate(detours):
-        routes.append((index, bits, begin, size))
-        begin += size
-
-    def detour(offset, route):
-        index, bits, begin, size = route
-        return remote(part_ref.at[offset, pl.ds(begin, size)],
-                      relay.at[offset, pl.ds(begin - half, size)], pass_send.at[offset, index],
-                      pass_recv.at[offset, index], (flip(x, bits), y))
-
-    def forward(offset, route, source):
-        index, bits, begin, size = route
-        return remote(relay.at[offset, pl.ds(begin - half, size)],
-                      arrived_ref.at[offset, pl.ds(begin - first, size)],
-                      fwd_send.at[offset, index], fwd_recv.at[offset, index],
-                      place(shifted(source, offset)))
-
-    def greet_route(offset, total):
-        here, there = hot(me, offset), hot(origin(offset), offset)
-        for _, bits, _, _ in routes:
-            source = flip(x, bits) * inner + y
+    def greet_flow(index, total):
+        away = reach - index // 2
+        offset = jnp.where(lax.rem(index, 2) == 0, reach + away, reach - away)
+        begun = origin(offset)
+        here, there = hot(me, offset), hot(begun, offset)
+
+        def greet_part(part, total):
+            source = beside(part) * inner + y
             middleman = hot(source, offset)
 
             @pl.when(here | middleman)
             def _():
-                greet((flip(x, bits), y))
+                greet((beside(part), y))
 
             @pl.when(middleman)
             def _():
@@ -309,42 +321,41 @@
 
             @pl.when(there)
             def _():
-                begun = origin(offset)
-                greet((flip(begun // inner, bits), lax.rem(begun, inner)))
-
-            total = (total + jnp.where(here | middleman, 1, 0) + jnp.where(middleman, 1, 0)
-                     + jnp.where(there, 1, 0))
-        return total
-
-    def greet_one(index, total):
-        away = reach - index // 2
-        return greet_route(jnp.where(lax.rem(index, 2) == 0, reach + away, reach - away), total)
-
-    pl.semaphore_wait(barrier, lax.fori_loop(0, 2 * reach, greet_one, 2 * reach))
+                greet((flip(begun // inner, part, outer), lax.rem(begun, inner)))
+
+            return (total + jnp.where(here | middleman, 1, 0) + jnp.where(middleman, 1, 0)
+                    + jnp.where(there, 1, 0))
+
+        return lax.fori_loop(1, parts, greet_part, total)
+
+    pl.semaphore_wait(barrier, lax.fori_loop(0, 2 * reach, greet_flow, 2 * reach))
 
     def start_hot(offset):
         @pl.when(hot(me, offset))
         def _():
-            for route in routes:
-                detour(offset, route).start()
+            each_part(lambda part: detour(offset, part).start())
             direct(offset).start()
 
         @pl.when(close(me, offset))
         def _():
             whole(offset).start()
 
-    def pass_on(offset):
-        for route in routes:
-            source = flip(x, route[1]) * inner + y
+    def middle(offset, act):
+        def one(part):
+            source = beside(part) * inner + y
 
             @pl.when(hot(source, offset))
-            def _(route=route, source=source):
-                detour(offset, route).wait_recv()
-                forward(offset, route, source).start()
+            def _():
+                act(offset, part, source)
+
+        each_part(one)
+
+    def pass_on(offset, part, source):
+        detour(offset, part).wait_recv()
+        forward(offset, part, source).start()
 
     def finish(offset):
-        early(offset).wait()
-        late(offset).wait()
+        repeat(0, 2, lambda step: base(offset, step).wait())
 
         @pl.when(close(me, offset))
         def _():
@@ -357,26 +368,24 @@
         @pl.when(hot(me, offset))
         def _():
             direct(offset).wait_send()
-            for route in routes:
-                detour(offset, route).wait_send()
+            each_part(lambda part: detour(offset, part).wait_send())
 
         @pl.when(hot(origin(offset), offset))
         def _():
             direct(offset).wait_recv()
-            for route in routes:
-                forward(offset, route, me).wait_recv()
-
-        for route in routes:
-            source = flip(x, route[1]) * inner + y
-
-            @pl.when(hot(source, offset))
-            def _(route=route, source=source):
-                forward(offset, route, source).wait_send()
+            each_part(lambda part: forward(offset, part, me).wait_recv())
+
+        middle(offset, lambda offset, part, source: forward(offset, part, source).wait_send())
+
+    def batch_step(step):
+        each_flow(lambda offset: base(offset, step).start())
+
+        @pl.when(step == 0)
+        def _():
+            each_flow(lambda offset: middle(offset, pass_on))
 
     each_flow(start_hot)
-    each_flow(lambda offset: early(offset).start())
-    each_flow(pass_on)
-    each_flow(lambda offset: late(offset).start())
+    repeat(0, 2, batch_step)
     each_flow(finish)
 
 
@@ -454,8 +463,8 @@
     columns = block_col.transpose(1, 0, 2)
     count = sizes[0] * sizes[1]
     half, first = slots // 2, slots // 4
-    share = (slots - half) // 8
-    detours = ((1, 2 * share), (2, 3 * share)) if sizes[0] % 4 == 0 else ()
+    parts = 4 if sizes[0] % 4 == 0 else 1
+    piece = (slots - half) // parts
     classes = min(count, MAX_CLASSES)
 
     vmem = pl.BlockSpec(memory_space=pltpu.VMEM)
@@ -521,14 +530,14 @@
     def rest(group):
         def call(part, arrived_meta, own, low):
             high = pl.pallas_call(
-                functools.partial(rest_kernel, axes, sizes, classes, group, first, half, detours),
+                functools.partial(rest_kernel, axes, sizes, classes, group, first, half, parts),
                 out_shape=pltpu.VMEM((num_off, slots - first, num_flux, block_rows),
                                      jnp.float32),
                 in_specs=[vmem],
                 out_specs=vmem,
                 scratch_shapes=[
-                    pltpu.VMEM((num_off, slots - half, num_flux, block_rows), jnp.float32),
-                ] + [dma((num_off,))] * 6 + [dma((num_off, max(len(detours), 1)))] * 4,
+                    pltpu.VMEM((num_off, parts, piece, num_flux, block_rows), jnp.float32),
+                ] + [dma((num_off, 2))] * 2 + [dma((num_off,))] * 2 + [dma((num_off, parts))] * 4,
                 compiler_params=pltpu.CompilerParams(
                     collective_id=classes + 1 if group is None else 1 + group,
                     has_side_effects=True, vmem_limit_bytes=16 * 2**20),

time: 73.8 us -> 73 us (0.989)
  no operation moved by 1% of the time
where the time goes in v3:
time: 73 us; the launch traced here: 72.1 us
  Pallas kernels  71 us (97%)
  between operations  0.82 us (1%)
    pallas_call x1, Pallas kernels, on_device(): pl.pallas_call(functools.partial(exchange_kernel, axes, sizes, classes, f...  34.5 us
    pallas_call x1, Pallas kernels, call(): pl.pallas_call(functools.partial(rest_kernel, axes, sizes, classes, group...  33.8 us
    pallas_call x1, Pallas kernels, settle(): pl.pallas_call(settle_kernel, out_shape=jax.ShapeDtypeStruct((num_kinds,...  2.75 us

profile of v3, /device:TPU:16, one launch (start us, length us, event | category | flops | bytes accessed | tf_op | source)
XLA Modules:
  0.0 72.1 jit_solution(2106726529885418507)
XLA Ops:
  0.0 34.5 %exchange.1 = (f32[7,16,48,256]{3,2,1,0:T(8,128)S(1)}, f32[16,48,256]{2,1,0:T(8,128)S(1)}, f32[7,4,48,256]{3,2,1,0:T(8,128)S(1)}, s32[7,2,1,16]{3,2,1,0:T(1,128)S(1)}, s32[1]{0:T(128)}) custom-call(bf16[4,12,8,4096]{3,2,1,0:T(8,128)(2,1)} %flux_ref.1, f32[8,4096]{1,0:T(8,128)} %frac_ref.1, s32[7,1,16]{2,1,0:T(1,128)} %bitcast.6, s32[1,7]{1,0:T(1,128)} %count_ref.1, ...), custom_call_target="tpu_custom_call" | custom-call | tf_op jit(solution)/shard_map/exchange/pallas_call | solution.py:475
  35.1 36.8 %conditional.1 = (f32[12,4,12288]{2,1,0:T(4,128)}) conditional(s32[]{:T(128)} %bitcast.3, (f32[7,16,48,256]{3,2,1,0:T(8,128)S(1)}, s32[7,2,1,16]{3,2,1,0:T(1,128)S(1)}, f32[16,48,256]{2,1,0:T(8,128)S(1)}, f32[7,4,48,256]{3,2,1,0:T(8,128)S(1)}) %tuple.104, (f32[7,16,48,256]{3,2,1,0:T(8,128)S(1)}, ...), branch_computations={%region_0.0_spmd, %region_1.0_spmd, %region_2.0_spmd, %region_3.0_... | conditional | bytes 8 | solution.py:550
  35.4 33.8 %rest.55.high_ref = f32[7,12,48,256]{3,2,1,0:T(8,128)S(1)} custom-call(f32[7,16,48,256]{3,2,1,0:T(8,128)S(1)} %get-tuple-element.394.part_ref), custom_call_target="tpu_custom_call" | custom-call | tf_op jit(solution)/shard_map/cond/branch_22_fun/rest/pallas_call | solution.py:532
  69.1 2.8 %settle.55 = f32[12,4,12288]{2,1,0:T(4,128)} custom-call(s32[7,2,1,16]{3,2,1,0:T(1,128)S(1)} %get-tuple-element.391.meta_ref, f32[16,48,256]{2,1,0:T(8,128)S(1)} %get-tuple-element.392.own_ref, f32[7,4,48,256]{3,2,1,0:T(8,128)S(1)} %get-tuple-element.393.low_ref, f32[7,12,48,256]{3,2,1,0:T(8,128)S(1)} %rest.55.high_ref), custom_call_target="tpu_custom_call" | custom-call | tf_op jit(solution)/shard_map/cond/branch_22_fun/settle/pallas_call | solution.py:513

commit v4 on v3

--- a/solution.py
+++ b/solution.py
@@ -85,29 +85,50 @@
     steps(outer, lambda step: greet((lax.rem(x + step, outer), y)))
     steps(inner, lambda step: greet((x, lax.rem(y + step, inner))))
 
-    land_loads = []
-    for block in range(flux_buf.shape[0]):
-        lanes = pl.ds(block * cols, cols)
-        land_loads.append(pltpu.make_async_copy(
-            flux_ref.at[:, :, :, lanes], flux_buf.at[block], flux_sem.at[block]))
-        land_loads.append(pltpu.make_async_copy(
-            frac_ref.at[:, lanes], frac_buf.at[block], frac_sem.at[block]))
-    for load in land_loads:
-        load.start()
-    meta_loads = [pltpu.make_async_copy(rows_ref.at[offset], meta.at[offset, 0],
-                                        meta_sem.at[offset]) for offset in range(num_off)]
-    for load in meta_loads:
-        load.start()
-    order = [(offset, span) for span in first_spans for offset in flow_order(reach)]
-    order += [(offset, span) for span in later_spans for offset in flow_order(reach)]
-    order += [(reach, (0, slots))]
-    loads = []
-    for index, (offset, span) in enumerate(order):
-        loads.append(pltpu.make_async_copy(
-            weights_ref.at[offset, pl.ds(*span)], weights_buf.at[offset, pl.ds(*span)],
-            weight_sem.at[index]))
-    for load in loads[:EARLY]:
-        load.start()
+    def repeat(begin, end, act):
+        def one(step, carry):
+            act(step)
+            return carry
+
+        lax.fori_loop(begin, end, one, 0)
+
+    def flow_offset(index):
+        away = reach - index // 2
+        return jnp.where(lax.rem(index, 2) == 0, reach + away, reach - away)
+
+    def land_loads(block):
+        lanes = pl.ds(pl.multiple_of(block * cols, cols), cols)
+        return (pltpu.make_async_copy(flux_ref.at[:, :, :, lanes], flux_buf.at[block],
+                                      flux_sem.at[block]),
+                pltpu.make_async_copy(frac_ref.at[:, lanes], frac_buf.at[block],
+                                      frac_sem.at[block]))
+
+    def start_land(block):
+        for load in land_loads(block):
+            load.start()
+
+    def wait_land(block):
+        for load in land_loads(block):
+            load.wait()
+
+    def meta_load(offset):
+        return pltpu.make_async_copy(rows_ref.at[offset], meta.at[offset, 0],
+                                     meta_sem.at[offset])
+
+    spans = first_spans + later_spans
+
+    def weight_load(offset, chunk):
+        span = pl.ds(*spans[chunk])
+        return pltpu.make_async_copy(weights_ref.at[offset, span], weights_buf.at[offset, span],
+                                     weight_sem.at[offset, chunk])
+
+    def own_load():
+        return pltpu.make_async_copy(weights_ref.at[reach], weights_buf.at[reach],
+                                     weight_sem.at[reach, 0])
+
+    repeat(0, flux_buf.shape[0], start_land)
+    repeat(0, num_off, lambda offset: meta_load(offset).start())
+    repeat(0, EARLY, lambda index: weight_load(flow_offset(index), 0).start())
 
     lane = lax.broadcasted_iota(jnp.int32, (1, LANES), 1)
     mine = lax.rem(me, classes)
@@ -121,10 +142,12 @@
             vote = jnp.where(fits, vote, 0)
     column_votes[x] = vote
 
-    for load in land_loads:
-        load.wait()
-    for load in loads[EARLY:]:
-        load.start()
+    repeat(0, flux_buf.shape[0], wait_land)
+    repeat(EARLY, 2 * reach, lambda index: weight_load(flow_offset(index), 0).start())
+    for chunk in range(1, len(spans)):
+        repeat(0, 2 * reach, lambda index, chunk=chunk: weight_load(
+            flow_offset(index), chunk).start())
+    own_load().start()
 
     def column_vote(step, source):
         return pltpu.make_async_remote_copy(
@@ -138,64 +161,80 @@
             send_sem=row_send_sem.at[step], recv_sem=row_recv_sem.at[step],
             device_id=(x, lax.rem(y + step, inner)), device_id_type=pl.DeviceIdType.MESH)
 
-    copies = []
-    for index, (offset, span) in enumerate(order):
-        begin, size = span
-        loads[index].wait()
-
-        def one_slot(slot, carry, offset=offset):
-            block = col_ref[offset, 0, slot]
-            frac = frac_buf[block]
-            flux = flux_buf[block].astype(jnp.float32)
-            flux = jnp.stack([flux[step] for step in range(num_steps)], axis=1)
-            flux = flux.reshape(num_steps * num_kinds, tiles, cols)
-            merged = jnp.sum(flux * frac[None], axis=1) / jnp.sum(frac, axis=0, keepdims=True)
-            value = lax.dot_general(
-                merged.astype(jnp.bfloat16), weights_buf[offset, slot],
-                (((1,), (1,)), ((), ())), preferred_element_type=jnp.float32)
-            if offset == reach:
-                own_ref[slot] = value
-            else:
-                part_ref[offset, slot] = value
+    def product(offset, slot):
+        block = col_ref[offset, 0, slot]
+        frac = frac_buf[block]
+        flux = flux_buf[block].astype(jnp.float32)
+        flux = jnp.stack([flux[step] for step in range(num_steps)], axis=1)
+        flux = flux.reshape(num_steps * num_kinds, tiles, cols)
+        merged = jnp.sum(flux * frac[None], axis=1) / jnp.sum(frac, axis=0, keepdims=True)
+        return lax.dot_general(merged.astype(jnp.bfloat16), weights_buf[offset, slot],
+                               (((1,), (1,)), ((), ())), preferred_element_type=jnp.float32)
+
+    def chunk_copy(offset, chunk):
+        span = pl.ds(*spans[chunk])
+        return pltpu.make_async_remote_copy(
+            src_ref=part_ref.at[offset, span], dst_ref=arrived_ref.at[offset, span],
+            send_sem=send_sem.at[offset, chunk], recv_sem=recv_sem.at[offset, chunk],
+            device_id=place(target(offset)), device_id_type=pl.DeviceIdType.MESH)
+
+    def meta_copy(offset):
+        return pltpu.make_async_remote_copy(
+            src_ref=meta.at[offset], dst_ref=arrived_meta_ref.at[offset],
+            send_sem=meta_send_sem.at[offset], recv_sem=meta_recv_sem.at[offset],
+            device_id=place(target(offset)), device_id_type=pl.DeviceIdType.MESH)
+
+    own_meta = pltpu.make_async_copy(meta.at[reach], arrived_meta_ref.at[reach], own_sem)
+
+    def store_slots(offset, chunk):
+        begin, size = spans[chunk]
+
+        def one_slot(slot, carry):
+            part_ref[offset, slot] = product(offset, slot)
             return carry
 
+        weight_load(offset, chunk).wait()
         lax.fori_loop(begin, begin + size, one_slot, 0, unroll=2 if size % 2 == 0 else 1)
-        if index == 0:
-            pl.semaphore_wait(barrier, greeted)
-        if span in first_spans and offset != reach:
-            chunk = first_spans.index(span)
-            copy = pltpu.make_async_remote_copy(
-                src_ref=part_ref.at[offset, pl.ds(begin, size)],
-                dst_ref=arrived_ref.at[offset, pl.ds(begin, size)],
-                send_sem=send_sem.at[offset, chunk], recv_sem=recv_sem.at[offset, chunk],
-                device_id=place(target(offset)), device_id_type=pl.DeviceIdType.MESH)
-            copy.start()
-            copies.append(copy)
-        if index == 0:
-            steps(outer, lambda step: column_vote(step, x).start())
-            for load in meta_loads:
-                load.wait()
-        if begin == 0:
-            if offset != reach:
-                copy = pltpu.make_async_remote_copy(
-                    src_ref=meta.at[offset], dst_ref=arrived_meta_ref.at[offset],
-                    send_sem=meta_send_sem.at[offset], recv_sem=meta_recv_sem.at[offset],
-                    device_id=place(target(offset)), device_id_type=pl.DeviceIdType.MESH)
-            else:
-                copy = pltpu.make_async_copy(
-                    meta.at[reach], arrived_meta_ref.at[reach], own_sem)
-            copy.start()
-            copies.append(copy)
-        if index == 4 * reach - 1:
+
+    def send_chunk(chunk, index):
+        offset = flow_offset(index)
+        store_slots(offset, chunk)
+        chunk_copy(offset, chunk).start()
+        if chunk == 0:
+            meta_copy(offset).start()
+
+    store_slots(2 * reach, 0)
+    repeat(0, num_off, lambda offset: meta_load(offset).wait())
+    pl.semaphore_wait(barrier, greeted)
+    chunk_copy(2 * reach, 0).start()
+    meta_copy(2 * reach).start()
+    own_meta.start()
+    steps(outer, lambda step: column_vote(step, x).start())
+    for chunk in range(len(first_spans)):
+        repeat(1 if chunk == 0 else 0, 2 * reach,
+               lambda index, chunk=chunk: send_chunk(chunk, index))
+        if chunk == min(1, len(first_spans) - 1):
             steps(outer, lambda step: column_vote(
                 step, lax.rem(x - step + outer, outer)).wait())
             row_votes[y] = jnp.min(column_votes[:, 0, :], axis=0, keepdims=True)
             steps(inner, lambda step: row_vote(step, y).start())
+    for chunk in range(len(first_spans), len(spans)):
+        repeat(0, 2 * reach, lambda index, chunk=chunk: store_slots(flow_offset(index), chunk))
+
+    def own_slot(slot, carry):
+        own_ref[slot] = product(reach, slot)
+        return carry
+
+    own_load().wait()
+    lax.fori_loop(0, slots, own_slot, 0, unroll=2)
     steps(inner, lambda step: row_vote(step, lax.rem(y - step + inner, inner)).wait())
     agreed = jnp.min(row_votes[:, 0, :], axis=0, keepdims=True)
     pick_ref[0] = jnp.min(jnp.where((agreed > 0) & (lane <= classes), lane, classes))
-    for copy in copies:
-        copy.wait()
+    own_meta.wait()
+    for chunk in range(len(first_spans)):
+        repeat(0, 2 * reach, lambda index, chunk=chunk: chunk_copy(
+            flow_offset(index), chunk).wait())
+    repeat(0, 2 * reach, lambda index: meta_copy(flow_offset(index)).wait())
 
 
 def rest_kernel(axes, sizes, classes, group, first, half, parts, part_ref, arrived_ref, relay,
@@ -261,32 +300,37 @@
     def each_part(act):
         repeat(1, parts, act)
 
-    def span(offset, begin, size, send, recv):
+    anyone = (lax.rem(x + 1, outer), y)
+
+    def toward(offset):
+        return place(shifted(me, offset))
+
+    def span(offset, begin, size, send, recv, device):
         return remote(part_ref.at[offset, pl.ds(begin, size)],
                       arrived_ref.at[offset, pl.ds(begin - first, size)],
-                      send, recv, place(shifted(me, offset)))
-
-    def base(offset, step):
+                      send, recv, device)
+
+    def base(offset, step, device=anyone):
         size = slots - first if group is None else batch
         return span(offset, first + step * batch, size, base_send.at[offset, step],
-                    base_recv.at[offset, step])
-
-    def direct(offset):
-        return span(offset, half, piece, send_sem.at[offset], recv_sem.at[offset])
-
-    def whole(offset):
-        return span(offset, half, slots - half, send_sem.at[offset], recv_sem.at[offset])
-
-    def detour(offset, part):
+                    base_recv.at[offset, step], device)
+
+    def direct(offset, device=anyone):
+        return span(offset, half, piece, send_sem.at[offset], recv_sem.at[offset], device)
+
+    def whole(offset, device=anyone):
+        return span(offset, half, slots - half, send_sem.at[offset], recv_sem.at[offset],
+                    device)
+
+    def detour(offset, part, device=anyone):
         return remote(part_ref.at[offset, pl.ds(half + part * piece, piece)],
                       relay.at[offset, part], pass_send.at[offset, part],
-                      pass_recv.at[offset, part], (beside(part), y))
-
-    def forward(offset, part, source):
+                      pass_recv.at[offset, part], device)
+
+    def forward(offset, part, device=anyone):
         return remote(relay.at[offset, part],
                       arrived_ref.at[offset, pl.ds(half - first + part * piece, piece)],
-                      fwd_send.at[offset, part], fwd_recv.at[offset, part],
-                      place(shifted(source, offset)))
+                      fwd_send.at[offset, part], fwd_recv.at[offset, part], device)
 
     barrier = pltpu.get_barrier_semaphore()
 
@@ -297,7 +341,7 @@
     each_flow(lambda offset: greet(place(shifted(me, offset))))
     if group is None:
         pl.semaphore_wait(barrier, 2 * reach)
-        each_flow(lambda offset: base(offset, 0).start())
+        each_flow(lambda offset: base(offset, 0, toward(offset)).start())
         each_flow(lambda offset: base(offset, 0).wait())
         return
 
@@ -333,12 +377,12 @@
     def start_hot(offset):
         @pl.when(hot(me, offset))
         def _():
-            each_part(lambda part: detour(offset, part).start())
-            direct(offset).start()
+            each_part(lambda part: detour(offset, part, (beside(part), y)).start())
+            direct(offset, toward(offset)).start()
 
         @pl.when(close(me, offset))
         def _():
-            whole(offset).start()
+            whole(offset, toward(offset)).start()
 
     def middle(offset, act):
         def one(part):
@@ -352,7 +396,7 @@
 
     def pass_on(offset, part, source):
         detour(offset, part).wait_recv()
-        forward(offset, part, source).start()
+        forward(offset, part, place(shifted(source, offset))).start()
 
     def finish(offset):
         repeat(0, 2, lambda step: base(offset, step).wait())
@@ -373,12 +417,12 @@
         @pl.when(hot(origin(offset), offset))
         def _():
             direct(offset).wait_recv()
-            each_part(lambda part: forward(offset, part, me).wait_recv())
-
-        middle(offset, lambda offset, part, source: forward(offset, part, source).wait_send())
+            each_part(lambda part: forward(offset, part).wait_recv())
+
+        middle(offset, lambda offset, part, source: forward(offset, part).wait_send())
 
     def batch_step(step):
-        each_flow(lambda offset: base(offset, step).start())
+        each_flow(lambda offset: base(offset, step, toward(offset)).start())
 
         @pl.when(step == 0)
         def _():
@@ -405,34 +449,37 @@
     lax.fori_loop(0, blocks, clear, 0, unroll=4)
     load.wait()
 
-    def add(offset, slot, value):
-        row = meta[offset, 0, 0, slot]
-        total[row] = total[row] + value
+    def add_pair(offset, slot, end, source, shift):
+        lone = slot + 1 >= end
+        other = jnp.where(lone, slot, slot + 1)
+        row, next_row = meta[offset, 0, 0, slot], meta[offset, 0, 0, other]
+        value, next_value = source(slot - shift), source(other - shift)
+        old, next_old = total[row], total[next_row]
+        new = old + value
+        kept = jnp.where(row == next_row, new, next_old)
+        total[row] = new
+        total[next_row] = jnp.where(lone, kept, kept + next_value)
+
+    def add_all(offset, begin, end, source, shift):
+        def one(pair, carry):
+            add_pair(offset, begin + 2 * pair, end, source, shift)
+            return carry
+
+        lax.fori_loop(0, (end - begin + 1) // 2, one, 0)
 
     def one_flow(offset, carry):
         live = meta[offset, 1, 0, 0]
 
-        def low_slot(slot, carry):
-            add(offset, slot, low_ref[offset, slot])
-            return carry
-
-        def high_slot(slot, carry):
-            add(offset, slot, high_ref[offset, slot - first])
-            return carry
-
         @pl.when(offset != reach)
         def _():
-            lax.fori_loop(0, jnp.minimum(live, first), low_slot, 0)
-            lax.fori_loop(first, live, high_slot, 0)
+            add_all(offset, 0, jnp.minimum(live, first), lambda slot: low_ref[offset, slot], 0)
+            add_all(offset, first, jnp.maximum(live, first),
+                    lambda slot: high_ref[offset, slot], first)
 
         return carry
 
-    def own_slot(slot, carry):
-        add(reach, slot, own_ref[slot])
-        return carry
-
     lax.fori_loop(0, num_off, one_flow, 0)
-    lax.fori_loop(0, meta[reach, 1, 0, 0], own_slot, 0)
+    add_all(reach, 0, meta[reach, 1, 0, 0], lambda slot: own_ref[slot], 0)
 
     per_cut = blocks // OUT_CUTS
     stores = []
@@ -471,7 +518,6 @@
     smem = pl.BlockSpec(memory_space=pltpu.SMEM)
     hbm = pl.BlockSpec(memory_space=pltpu.HBM)
     dma = pltpu.SemaphoreType.DMA
-    steps = 2 * slots * num_off
     part, own, low, arrived_meta, pick = pl.pallas_call(
         functools.partial(exchange_kernel, axes, sizes, classes, first, half),
         out_shape=(
@@ -492,7 +538,7 @@
             pltpu.VMEM((sizes[1], 1, LANES), jnp.int32),
             dma((land_blocks,)),
             dma((land_blocks,)),
-            dma((steps,)),
+            dma((num_off, slots)),
             dma((num_off,)),
             dma,
             dma((num_off, first)),

time: 73 us -> 74.8 us (1.025); the launches traced: 72.1 us -> 75.1 us
  Pallas kernels: 71 us -> 73.7 us
    pallas_call x1, Pallas kernels: 33.8 us -> 36.7 us  [call(): pl.pallas_call(functools.partial(rest_kernel, axes, sizes, classes, group...]
    pallas_call x1, Pallas kernels: 34.5 us -> 33.5 us  [on_device(): pl.pallas_call(functools.partial(exchange_kernel, axes, sizes, classes, f...]
where the time goes in v4:
time: 74.8 us; the launch traced here: 75.1 us
  Pallas kernels  73.7 us (99%)
  between operations  0.86 us (1%)
    pallas_call x1, Pallas kernels, call(): pl.pallas_call(functools.partial(rest_kernel, axes, sizes, classes, group...  36.7 us
    pallas_call x1, Pallas kernels, on_device(): pl.pallas_call(functools.partial(exchange_kernel, axes, sizes, classes, f...  33.5 us
    pallas_call x1, Pallas kernels, settle(): pl.pallas_call(settle_kernel, out_shape=jax.ShapeDtypeStruct((num_kinds,...  3.45 us

profile of v4, /device:TPU:16, one launch (start us, length us, event | category | flops | bytes accessed | tf_op | source)
XLA Modules:
  0.0 75.1 jit_solution(10094894696850653423)
XLA Ops:
  0.0 33.5 %exchange.1 = (f32[7,16,48,256]{3,2,1,0:T(8,128)S(1)}, f32[16,48,256]{2,1,0:T(8,128)S(1)}, f32[7,4,48,256]{3,2,1,0:T(8,128)S(1)}, s32[7,2,1,16]{3,2,1,0:T(1,128)S(1)}, s32[1]{0:T(128)}) custom-call(bf16[4,12,8,4096]{3,2,1,0:T(8,128)(2,1)} %flux_ref.1, f32[8,4096]{1,0:T(8,128)} %frac_ref.1, s32[7,1,16]{2,1,0:T(1,128)} %bitcast.6, s32[1,7]{1,0:T(1,128)} %count_ref.1, ...), custom_call_target="tpu_custom_call" | custom-call | tf_op jit(solution)/shard_map/exchange/pallas_call | solution.py:521
  34.2 40.8 %conditional.1 = (f32[12,4,12288]{2,1,0:T(4,128)}) conditional(s32[]{:T(128)} %bitcast.3, (f32[7,16,48,256]{3,2,1,0:T(8,128)S(1)}, s32[7,2,1,16]{3,2,1,0:T(1,128)S(1)}, f32[16,48,256]{2,1,0:T(8,128)S(1)}, f32[7,4,48,256]{3,2,1,0:T(8,128)S(1)}) %tuple.104, (f32[7,16,48,256]{3,2,1,0:T(8,128)S(1)}, ...), branch_computations={%region_0.0_spmd, %region_1.0_spmd, %region_2.0_spmd, %region_3.0_... | conditional | bytes 8 | solution.py:596
  34.2 36.7 %rest.37.high_ref = f32[7,12,48,256]{3,2,1,0:T(8,128)S(1)} custom-call(f32[7,16,48,256]{3,2,1,0:T(8,128)S(1)} %get-tuple-element.310.part_ref), custom_call_target="tpu_custom_call" | custom-call | tf_op jit(solution)/shard_map/cond/branch_4_fun/rest/pallas_call | solution.py:578
  70.9 3.5 %settle.37 = f32[12,4,12288]{2,1,0:T(4,128)} custom-call(s32[7,2,1,16]{3,2,1,0:T(1,128)S(1)} %get-tuple-element.302.meta_ref, f32[16,48,256]{2,1,0:T(8,128)S(1)} %get-tuple-element.303.own_ref, f32[7,4,48,256]{3,2,1,0:T(8,128)S(1)} %get-tuple-element.304.low_ref, f32[7,12,48,256]{3,2,1,0:T(8,128)S(1)} %rest.37.high_ref), custom_call_target="tpu_custom_call" | custom-call | tf_op jit(solution)/shard_map/cond/branch_4_fun/settle/pallas_call | solution.py:559
